TPU v7x, 32 devices: a whole 2x2x4 slice. The times are simulated.
32 devices in a mesh: row: 16 (over z, y, x), col: 2 (over core).
Axes of the slice: x: 2, y: 2, z: 4, core: 2. Of those that a mesh axis runs over, the one named last changes fastest.
Arguments:
- tokens: bfloat16 [16400, 1024], P('row', 'col'), may hold values from -6 to 6
- norm1_gain: bfloat16 [1024], P('row'), may hold values from 0.099609375 to 1.8984375
- norm1_bias: bfloat16 [1024], P('row'), may hold values from -1.75 to 1.75
- qkv_weight: bfloat16 [1024, 3, 1024], P('row', None, 'col'), may hold values from -0.1875 to 0.1875
- query_bias: bfloat16 [1024], P('col'), may hold values from -1.75 to 1.75
- value_bias: bfloat16 [1024], P('col'), may hold values from -0.3125 to 0.3125
- proj_weight: bfloat16 [1024, 1024], P('col', 'row'), may hold values from -6 to 6
- proj_bias: bfloat16 [1024], P('row'), may hold values from -1.75 to 1.75
- norm2_gain: bfloat16 [1024], P('row'), may hold values from 0.099609375 to 1.8984375
- norm2_bias: bfloat16 [1024], P('row'), may hold values from -1.75 to 1.75
- gate_weight: bfloat16 [1024, 2730], P('row', 'col'), may hold values from -0.1875 to 0.1875
- gate_bias: bfloat16 [2730], P('col'), may hold values from -1.75 to 1.75
- up_weight: bfloat16 [1024, 2730], P('row', 'col'), may hold values from -0.1875 to 0.1875
- up_bias: bfloat16 [2730], P('col'), may hold values from -1.75 to 1.75
- inner_gain: bfloat16 [2730], P('col'), may hold values from 0.099609375 to 1.8984375
- inner_bias: bfloat16 [2730], P('col'), may hold values from -1.75 to 1.75
- down_weight: bfloat16 [2730, 1024], P('col', 'row'), may hold values from -0.109375 to 0.109375
- down_bias: bfloat16 [1024], P('row'), may hold values from -1.75 to 1.75
- cotangent: bfloat16 [16400, 1024], P('row', 'col'), may hold values from -6 to 6
Outputs:
- layer_out: bfloat16 [16400, 1024], P('row', 'col')
- input_grad: bfloat16 [16400, 1024], P('row', 'col')
- norm1_gain_grad: float32 [1024], P('row')
- norm1_bias_grad: float32 [1024], P('row')
- qkv_weight_grad: float32 [1024, 3, 1024], P('row', None, 'col')
- query_bias_grad: float32 [1024], P('col')
- value_bias_grad: float32 [1024], P('col')
- proj_weight_grad: float32 [1024, 1024], P('col', 'row')
- proj_bias_grad: float32 [1024], P('row')
- norm2_gain_grad: float32 [1024], P('row')
- norm2_bias_grad: float32 [1024], P('row')
- gate_weight_grad: float32 [1024, 2730], P('row', 'col')
- gate_bias_grad: float32 [2730], P('col')
- up_weight_grad: float32 [1024, 2730], P('row', 'col')
- up_bias_grad: float32 [2730], P('col')
- inner_gain_grad: float32 [2730], P('col')
- inner_bias_grad: float32 [2730], P('col')
- down_weight_grad: float32 [2730, 1024], P('col', 'row')
- down_bias_grad: float32 [1024], P('row')
All inputs are finite; a program needn't handle non-finite values.
Results may differ from a plain program's by a relative error of at most 0.023.
Values may be sent and summed in bfloat16 or wider, within the bound.
A program may use at most 192 MiB of HBM per device.

v0:
```python
import math

import jax
import jax.numpy as jnp
from jax import lax
from jax.sharding import PartitionSpec as P

HD = 64
FF = 2730
GRID = 32
SEQ = 1025


EPSILON = 1e-06


def norm_forward(values, norm_gain, norm_shift):
    row_mean = jnp.mean(values, axis=-1, keepdims=True)
    centred = values - row_mean
    variance = jnp.mean(centred * centred, axis=-1, keepdims=True)
    inv_std = lax.rsqrt(variance + EPSILON)
    normed = centred * inv_std
    return (normed * norm_gain + norm_shift, normed, inv_std)


def norm_backward(upstream, normed, inv_std, norm_gain):
    scaled = upstream * norm_gain
    first_mean = jnp.mean(scaled, axis=-1, keepdims=True)
    second_mean = jnp.mean(scaled * normed, axis=-1, keepdims=True)
    delta = inv_std * (scaled - first_mean - normed * second_mean)
    return (delta, jnp.sum(upstream * normed, axis=0), jnp.sum(upstream, axis=0))


def rotary_tables(length, seq_len, grid_side, head_size):
    quarter = head_size // 4
    position = jnp.arange(length, dtype=jnp.int32) % seq_len
    patch_index = jnp.maximum(position - 1, 0)
    inside = (position > 0).astype(jnp.float32)
    row_pos = (patch_index // grid_side).astype(jnp.float32) * inside
    col_pos = (patch_index % grid_side).astype(jnp.float32) * inside
    frequency = jnp.exp(-math.log(10000.0) * jnp.arange(quarter, dtype=jnp.float32) / quarter)
    row_angle = row_pos[:, None] * frequency[None, :]
    col_angle = col_pos[:, None] * frequency[None, :]
    angles = jnp.concatenate([row_angle, row_angle, col_angle, col_angle], axis=1)
    return (jnp.cos(angles), jnp.sin(angles))


def rotate(values):
    pieces = jnp.split(values, 4, axis=-1)
    return jnp.concatenate([-pieces[1], pieces[0], -pieces[3], pieces[2]], axis=-1)


def rotate_transposed(values):
    pieces = jnp.split(values, 4, axis=-1)
    return jnp.concatenate([pieces[1], -pieces[0], pieces[3], -pieces[2]], axis=-1)


def apply_rotary(values, cosine_table, sine_table):
    return values * cosine_table[:, None, :] + rotate(values) * sine_table[:, None, :]


def rotary_back(grads, cosine_table, sine_table):
    return grads * cosine_table[:, None, :] + rotate_transposed(grads * sine_table[:, None, :])


def own_half(vector, column, half_width):
    return lax.dynamic_slice_in_dim(vector, column * half_width, half_width, axis=vector.ndim - 1)


def share_columns(partial_sums):
    return lax.psum_scatter(
        partial_sums.astype(jnp.bfloat16), "col", scatter_dimension=1, tiled=True
    ).astype(jnp.float32)


def join_columns(partial_sums):
    return lax.psum(partial_sums.astype(jnp.bfloat16), "col").astype(jnp.float32)


def hidden_totals(row_sums):
    return lax.psum(row_sums, "col")


def body(
    tokens,
    norm1_gain,
    norm1_bias,
    qkv_weight,
    query_bias,
    value_bias,
    proj_weight,
    proj_bias,
    norm2_gain,
    norm2_bias,
    gate_weight,
    gate_bias,
    up_weight,
    up_bias,
    inner_gain,
    inner_bias,
    down_weight,
    down_bias,
    cotangent,
):
    single = jnp.float32
    narrow = jnp.bfloat16
    local_rows = tokens.shape[0]
    half_width = tokens.shape[1]
    head_local = half_width // HD
    images_local = local_rows // SEQ
    column = lax.axis_index("col")
    scaling = 1.0 / math.sqrt(HD)
    cosine_table, sine_table = rotary_tables(local_rows, SEQ, GRID, HD)

    def by_head(array):
        shaped = array.reshape(images_local, SEQ, head_local, HD).transpose(0, 2, 1, 3)
        return shaped.reshape(images_local * head_local, SEQ, HD)

    def from_head(array):
        shaped = array.reshape(images_local, head_local, SEQ, HD).transpose(0, 2, 1, 3)
        return shaped.reshape(local_rows, half_width)

    qkv_full, proj_full, attn_vectors = (
        lax.all_gather(qkv_weight, "row", axis=0, tiled=True),
        lax.all_gather(proj_weight, "row", axis=1, tiled=True),
        lax.all_gather(jnp.stack([norm1_gain, norm1_bias, proj_bias]), "row", axis=1, tiled=True),
    )
    whole_input = lax.all_gather(tokens, "col", axis=1, tiled=True).astype(single)
    normed_out, normed_one, inv_std_one = norm_forward(
        whole_input, attn_vectors[0].astype(single), attn_vectors[1].astype(single)
    )
    first_input = normed_out.astype(narrow)
    qkv_bias = jnp.stack(
        [query_bias.astype(single), jnp.zeros((half_width,), single), value_bias.astype(single)]
    )
    projected = (
        jnp.einsum("td,dpe->tpe", first_input, qkv_full, preferred_element_type=single) + qkv_bias
    )
    queries = apply_rotary(
        projected[:, 0].reshape(local_rows, head_local, HD), cosine_table, sine_table
    ).astype(narrow)
    keys_all = apply_rotary(
        projected[:, 1].reshape(local_rows, head_local, HD), cosine_table, sine_table
    ).astype(narrow)
    values_all = projected[:, 2].astype(narrow)

    def attend(operands):
        query_block, key_block, value_block = operands
        scores = (
            jnp.einsum("qd,kd->qk", query_block, key_block, preferred_element_type=single) * scaling
        )
        weights = jax.nn.softmax(scores, axis=-1)
        mixed = jnp.einsum(
            "qk,kd->qd", weights.astype(narrow), value_block, preferred_element_type=single
        )
        return mixed.astype(narrow)

    attended = from_head(
        lax.map(attend, (by_head(queries), by_head(keys_all), by_head(values_all)))
    )
    attn_partial = jnp.dot(attended, proj_full, preferred_element_type=single)
    residual_half = (
        tokens.astype(single)
        + share_columns(attn_partial)
        + own_half(attn_vectors[2].astype(single), column, half_width)
    )
    residual_full = lax.all_gather(
        residual_half.astype(jnp.bfloat16), "col", axis=1, tiled=True
    ).astype(residual_half.dtype)
    gate_full, up_full, down_full, ffn_vectors = (
        lax.all_gather(gate_weight, "row", axis=0, tiled=True),
        lax.all_gather(up_weight, "row", axis=0, tiled=True),
        lax.all_gather(down_weight, "row", axis=1, tiled=True),
        lax.all_gather(jnp.stack([norm2_gain, norm2_bias, down_bias]), "row", axis=1, tiled=True),
    )
    second_out, normed_two, inv_std_two = norm_forward(
        residual_full, ffn_vectors[0].astype(single), ffn_vectors[1].astype(single)
    )
    second_input = second_out.astype(narrow)
    gate_value = jnp.dot(second_input, gate_full, preferred_element_type=single) + gate_bias.astype(
        single
    )
    up_value = jnp.dot(second_input, up_full, preferred_element_type=single) + up_bias.astype(
        single
    )
    sigmoid_gate = jax.nn.sigmoid(gate_value)
    hidden = gate_value * sigmoid_gate * up_value
    hidden_mean = hidden_totals((jnp.sum(hidden, axis=1),))[0][:, None] / FF
    hidden_centred = hidden - hidden_mean
    hidden_var = hidden_totals((jnp.sum(hidden_centred * hidden_centred, axis=1),))[0][:, None] / FF
    hidden_inv = lax.rsqrt(hidden_var + EPSILON)
    hidden_normed = hidden_centred * hidden_inv
    down_input = (hidden_normed * inner_gain.astype(single) + inner_bias.astype(single)).astype(
        narrow
    )
    ffn_partial = jnp.dot(down_input, down_full, preferred_element_type=single)
    layer_out = (
        residual_half
        + share_columns(ffn_partial)
        + own_half(ffn_vectors[2].astype(single), column, half_width)
    ).astype(narrow)
    out_full = lax.all_gather(cotangent, "col", axis=1, tiled=True)
    out_float = out_full.astype(single)
    gate_back, up_back, down_back, ffn_back_vectors = (
        lax.all_gather(gate_weight, "row", axis=0, tiled=True),
        lax.all_gather(up_weight, "row", axis=0, tiled=True),
        lax.all_gather(down_weight, "row", axis=1, tiled=True),
        lax.all_gather(jnp.stack([norm2_gain, norm2_bias, down_bias]), "row", axis=1, tiled=True),
    )
    down_weight_grad = jnp.einsum("tf,td->fd", down_input, out_full, preferred_element_type=single)
    down_bias_grad = jnp.sum(out_float, axis=0)
    normed_grad = jnp.einsum("td,fd->tf", out_full, down_back, preferred_element_type=single)
    scaled_grad = normed_grad * inner_gain.astype(single)
    first_total, second_total = hidden_totals(
        (jnp.sum(scaled_grad, axis=1), jnp.sum(scaled_grad * hidden_normed, axis=1))
    )
    hidden_grad = hidden_inv * (
        scaled_grad - first_total[:, None] / FF - hidden_normed * (second_total[:, None] / FF)
    )
    inner_gain_grad = jnp.sum(normed_grad * hidden_normed, axis=0)
    inner_bias_grad = jnp.sum(normed_grad, axis=0)
    gate_grad = (
        hidden_grad * up_value * sigmoid_gate * (1.0 + gate_value * (1.0 - sigmoid_gate))
    ).astype(narrow)
    up_grad = (hidden_grad * gate_value * sigmoid_gate).astype(narrow)
    gate_bias_grad = jnp.sum(gate_grad.astype(single), axis=0)
    up_bias_grad = jnp.sum(up_grad.astype(single), axis=0)
    gate_weight_grad = jnp.einsum(
        "td,tf->df", second_input, gate_grad, preferred_element_type=single
    )
    up_weight_grad = jnp.einsum("td,tf->df", second_input, up_grad, preferred_element_type=single)
    second_back = join_columns(
        jnp.einsum("tf,df->td", gate_grad, gate_back, preferred_element_type=single)
        + jnp.einsum("tf,df->td", up_grad, up_back, preferred_element_type=single)
    )
    second_delta, gain_two_grad, shift_two_grad = norm_backward(
        second_back, normed_two, inv_std_two, ffn_back_vectors[0].astype(single)
    )
    residual_grad = out_float + second_delta
    ffn_vector_grads = jnp.stack([gain_two_grad, shift_two_grad, down_bias_grad])
    ffn_sums = (
        lax.psum_scatter(gate_weight_grad, "row", scatter_dimension=0, tiled=True),
        lax.psum_scatter(up_weight_grad, "row", scatter_dimension=0, tiled=True),
        lax.psum_scatter(down_weight_grad, "row", scatter_dimension=1, tiled=True),
        lax.psum_scatter(ffn_vector_grads, "row", scatter_dimension=1, tiled=True),
    )
    qkv_back, proj_back, attn_back_vectors = (
        lax.all_gather(qkv_weight, "row", axis=0, tiled=True),
        lax.all_gather(proj_weight, "row", axis=1, tiled=True),
        lax.all_gather(jnp.stack([norm1_gain, norm1_bias, proj_bias]), "row", axis=1, tiled=True),
    )
    attn_grad = residual_grad.astype(narrow)
    proj_bias_grad = jnp.sum(attn_grad.astype(single), axis=0)
    proj_weight_grad = jnp.einsum("te,td->ed", attended, attn_grad, preferred_element_type=single)
    attended_grad = jnp.einsum(
        "td,ed->te", attn_grad, proj_back, preferred_element_type=single
    ).astype(narrow)

    def attend_back(operands):
        query_block, key_block, value_block, grad_block = operands
        scores = (
            jnp.einsum("qd,kd->qk", query_block, key_block, preferred_element_type=single) * scaling
        )
        weights = jax.nn.softmax(scores, axis=-1)
        value_grad = jnp.einsum(
            "qk,qd->kd", weights.astype(narrow), grad_block, preferred_element_type=single
        )
        weight_grad = jnp.einsum(
            "qd,kd->qk", grad_block, value_block, preferred_element_type=single
        )
        score_grad = (
            weights * (weight_grad - jnp.sum(weight_grad * weights, axis=-1, keepdims=True))
        ).astype(narrow)
        query_grad = (
            jnp.einsum("qk,kd->qd", score_grad, key_block, preferred_element_type=single) * scaling
        )
        key_grad = (
            jnp.einsum("qk,qd->kd", score_grad, query_block, preferred_element_type=single)
            * scaling
        )
        return (query_grad, key_grad, value_grad)

    query_grads, key_grads, value_grads = lax.map(
        attend_back,
        (by_head(queries), by_head(keys_all), by_head(values_all), by_head(attended_grad)),
    )
    query_pre = rotary_back(
        from_head(query_grads).reshape(local_rows, head_local, HD), cosine_table, sine_table
    )
    key_pre = rotary_back(
        from_head(key_grads).reshape(local_rows, head_local, HD), cosine_table, sine_table
    )
    qkv_grad = jnp.stack(
        [
            query_pre.reshape(local_rows, half_width),
            key_pre.reshape(local_rows, half_width),
            from_head(value_grads),
        ],
        axis=1,
    ).astype(narrow)
    qkv_grad_float = qkv_grad.astype(single)
    query_bias_grad = jnp.sum(qkv_grad_float[:, 0], axis=0)
    value_bias_grad = jnp.sum(qkv_grad_float[:, 2], axis=0)
    qkv_weight_grad = jnp.einsum(
        "td,tpe->dpe", first_input, qkv_grad, preferred_element_type=single
    )
    first_back = join_columns(
        jnp.einsum("tpe,dpe->td", qkv_grad, qkv_back, preferred_element_type=single)
    )
    first_delta, gain_one_grad, shift_one_grad = norm_backward(
        first_back, normed_one, inv_std_one, attn_back_vectors[0].astype(single)
    )
    input_grad = own_half(residual_grad + first_delta, column, half_width).astype(narrow)
    attn_vector_grads = jnp.stack([gain_one_grad, shift_one_grad, proj_bias_grad])
    attn_sums = (
        lax.psum_scatter(qkv_weight_grad, "row", scatter_dimension=0, tiled=True),
        lax.psum_scatter(proj_weight_grad, "row", scatter_dimension=1, tiled=True),
        lax.psum_scatter(attn_vector_grads, "row", scatter_dimension=1, tiled=True),
    )
    small_sums = lax.psum(
        (
            jnp.stack([query_bias_grad, value_bias_grad]),
            jnp.stack([gate_bias_grad, up_bias_grad, inner_gain_grad, inner_bias_grad]),
        ),
        "row",
    )
    return (
        layer_out,
        input_grad,
        attn_sums[2][0],
        attn_sums[2][1],
        attn_sums[0],
        small_sums[0][0],
        small_sums[0][1],
        attn_sums[1],
        attn_sums[2][2],
        ffn_sums[3][0],
        ffn_sums[3][1],
        ffn_sums[0],
        small_sums[1][0],
        ffn_sums[1],
        small_sums[1][1],
        small_sums[1][2],
        small_sums[1][3],
        ffn_sums[2],
        ffn_sums[3][2],
    )


def solution(mesh):
    placed = (
        P("row", "col"),
        P("row"),
        P("row"),
        P("row", None, "col"),
        P("col"),
        P("col"),
        P("col", "row"),
        P("row"),
        P("row"),
        P("row"),
        P("row", "col"),
        P("col"),
        P("row", "col"),
        P("col"),
        P("col"),
        P("col"),
        P("col", "row"),
        P("row"),
        P("row", "col"),
    )
    return jax.shard_map(
        body,
        mesh=mesh,
        in_specs=placed,
        out_specs=(
            P("row", "col"),
            P("row", "col"),
            P("row"),
            P("row"),
            P("row", None, "col"),
            P("col"),
            P("col"),
            P("col", "row"),
            P("row"),
            P("row"),
            P("row"),
            P("row", "col"),
            P("col"),
            P("row", "col"),
            P("col"),
            P("col"),
            P("col"),
            P("col", "row"),
            P("row"),
        ),
        check_vma=False,
    )
```

profile of v0, /device:TPU:0, one launch (start us, length us, event | category | flops | bytes accessed | tf_op | source)
XLA Modules:
  0.0 1409.8 jit_solution(9461431110204943578)
XLA Ops:
  11.6 42.5 %all-gather = bf16[16,64,3]{1,2,0:T(4,128)(2,1)S(1)} all-gather(bf16[1,64,3]{1,2,0:T(4,128)(2,1)S(1)} %maximum_bitcast_fusion), channel_id=1, replica_groups=mesh['row'=16,'col'=2] {'row'}, dimensions={0}, use_global_device_ids=true | all-gather | bytes 6528 | tf_op jit(solution)/shard_map/all_gather | solution.py:126
  59.3 35.4 %all-gather.13.cloned.1.call-done = bf16[1024,3,512]{2,0,1:T(8,128)(2,1)} async-done(((bf16[64,3,512]{2,0,1:T(8,128)(2,1)}), bf16[1024,3,512]{2,0,1:T(8,128)(2,1)}) %all-gather.13.cloned.1.call-update) | async-done | bytes 3145744 | tf_op jit(solution)/shard_map/all_gather | solution.py:124
  94.7 5.9 convolution_add_fusion.2
  106.3 3.0 copy.81
  113.4 2.9 copy.86
  122.7 41.4 %while.24 = (s32[]{:T(128)}, bf16[8,1025,64]{1,2,0:T(8,128)(2,1)}, bf16[8,1025,64]{2,1,0:T(8,128)(2,1)S(1)}, bf16[8,1025,64]{2,1,0:T(8,128)(2,1)}, bf16[8,1025,64]{2,1,0:T(8,128)(2,1)}, /*index=5*/s32[]{:T(128)}) while((s32[]{:T(128)}, bf16[8,1025,64]{1,2,0:T(8,128)(2,1)}, bf16[8,1025,64]{2,1,0:T(8,128)(2,1)S(1)}, ...), condition=%wide.region_5.6_spmd, body=%wide.region_2.5_spmd.sunk | while | flops 276377920 | bytes 13570157 | solution.py:159
  125.3 2.6 fusion.165
  164.1 5.3 convolution_convert_fusion.1
  169.7 8.1 reduce-scatter.14.cloned.1.call-done
  183.4 41.0 %all-gather.1 = bf16[16,64,3]{1,2,0:T(4,128)(2,1)S(1)} all-gather(bf16[1,64,3]{1,2,0:T(4,128)(2,1)S(1)} %maximum_bitcast_fusion.1), channel_id=1, replica_groups=mesh['row'=16,'col'=2] {'row'}, dimensions={0}, use_global_device_ids=true | all-gather | bytes 6528 | tf_op jit(solution)/shard_map/all_gather | solution.py:174
  228.2 34.2 %all-gather.19.cloned.1.call-done = bf16[1024,1365]{1,0:T(8,128)(2,1)} async-done(((bf16[64,1365]{1,0:T(8,128)(2,1)}), bf16[1024,1365]{1,0:T(8,128)(2,1)}) %all-gather.19.cloned.1.call-update) | async-done | bytes 2795536 | tf_op jit(solution)/shard_map/all_gather | solution.py:171
  262.4 7.8 convolution_add_fusion.1
  270.2 59.7 %all-gather.21.cloned.1.call-done = bf16[1024,1365]{1,0:T(8,128)(2,1)} async-done(((bf16[64,1365]{1,0:T(8,128)(2,1)}), bf16[1024,1365]{1,0:T(8,128)(2,1)}) %all-gather.21.cloned.1.call-update) | async-done | bytes 2795536 | tf_op jit(solution)/shard_map/all_gather | solution.py:172
  329.9 10.2 fusion.115
  342.6 3.4 multiply_reduce_fusion.3
  348.5 62.1 %all-gather.23.cloned.1.call-done = bf16[1365,1024]{0,1:T(8,128)(2,1)} async-done(((bf16[1365,64]{0,1:T(8,128)(2,1)}), bf16[1365,1024]{0,1:T(8,128)(2,1)}) %all-gather.23.cloned.1.call-update) | async-done | bytes 2795536 | tf_op jit(solution)/shard_map/all_gather | solution.py:173
  410.7 11.1 multiply_reduce_fusion.1
  421.8 3.3 all-reduce.1
  425.1 11.1 convert_reduce_fusion.2
  436.2 3.5 fusion.126
  440.2 4.7 fusion.67
  446.5 11.5 copy.96
  458.0 7.1 all-reduce.5.cloned.1.call-done
  465.1 3.6 fusion.64
  475.8 100.6 %while.25 = (s32[]{:T(128)}, f32[8,1025,64]{1,2,0:T(8,128)S(1)}, f32[8,1025,64]{1,2,0:T(8,128)}, bf16[8,1025,64]{1,2,0:T(8,128)(2,1)}, bf16[8,1025,64]{2,1,0:T(8...) while((s32[]{:T(128)}, f32[8,1025,64]{1,2,0:T(8,128)S(1)}, ...), condition=%wide.region_25.26_spmd, body=%wide.region_21.25_spmd.sunk | while | flops 689338112 | bytes 38548656 | solution.py:283
  576.5 3.1 copy.101
  579.6 3.4 bitcast_multiply_fusion.1
  585.2 3.2 copy.95
  590.7 3.3 copy.98
  594.0 4.9 add_convert_fusion.3
  599.9 4.8 fusion.66
  606.0 8.5 convolution_convert_fusion
  614.6 12.9 all-reduce.7.cloned.1.call-done
  627.4 6.4 fusion.65
  635.0 5.7 fusion.102
  640.8 8.7 fusion.111
  649.6 8.2 fusion.109
  659.4 9.2 fusion.106
  670.2 8.9 fusion.86
  681.5 77.1 %all-reduce = (f32[2,512]{1,0:T(2,128)S(1)}, f32[4,1365]{1,0:T(4,128)S(1)}) all-reduce(f32[2,512]{1,0:T(2,128)S(1)} %pad_maximum_fusion.8, f32[4,1365]{1,0:T(4,128)S(1)} %pad_maximum_fusion.4), channel_id=1, replica_groups=mesh['row'=16,'col'=2] {'row'}, use_global_device_ids=true, to_apply=%region_36.37 | all-reduce | flops 6484 | bytes 51872 | tf_op jit(solution)/shard_map/psum | solution.py:320
  762.6 4.5 fusion.73
  767.1 2.7 add_convert_fusion.4
  769.8 27.7 %reduce-scatter.28.cloned.1.call-done = f32[64,3]{1,0:T(8,128)} async-done(((f32[1024,3]{1,0:T(8,128)}), f32[64,3]{1,0:T(8,128)}) %reduce-scatter.28.cloned.1.call-update) | async-done | bytes 784
  800.2 77.9 %reduce-scatter.20.cloned.1.call-done = f32[512,64]{0,1:T(8,128)} async-done(((f32[512,1024]{0,1:T(8,128)}), f32[512,64]{0,1:T(8,128)}) %reduce-scatter.20.cloned.1.call-update) | async-done | bytes 131088 | tf_op jit(solution)/shard_map/reduce_scatter | solution.py:317
  878.1 124.6 %reduce-scatter.22.cloned.1.call-done = f32[64,1365]{1,0:T(8,128)} async-done(((f32[1024,1365]{1,0:T(8,128)}), f32[64,1365]{1,0:T(8,128)}) %reduce-scatter.22.cloned.1.call-update) | async-done | bytes 349456 | tf_op jit(solution)/shard_map/reduce_scatter | solution.py:242
  1002.8 130.4 %reduce-scatter.24.cloned.1.call-done = f32[64,1365]{1,0:T(8,128)} async-done(((f32[1024,1365]{1,0:T(8,128)}), f32[64,1365]{1,0:T(8,128)}) %reduce-scatter.24.cloned.1.call-update) | async-done | bytes 349456 | tf_op jit(solution)/shard_map/reduce_scatter | solution.py:243
  1133.2 129.8 %reduce-scatter.26.cloned.1.call-done = f32[1365,64]{0,1:T(8,128)} async-done(((f32[1365,1024]{0,1:T(8,128)}), f32[1365,64]{0,1:T(8,128)}) %reduce-scatter.26.cloned.1.call-update) | async-done | bytes 349456 | tf_op jit(solution)/shard_map/reduce_scatter | solution.py:244
  1263.0 140.1 %reduce-scatter.18.cloned.1.call-done = f32[64,3,512]{2,0,1:T(8,128)} async-done(((f32[1024,3,512]{2,0,1:T(8,128)}), f32[64,3,512]{2,0,1:T(8,128)}) %reduce-scatter.18.cloned.1.call-update) | async-done | bytes 393232 | tf_op jit(solution)/shard_map/reduce_scatter | solution.py:316
  (344 shorter events, 208.5 us)
Async XLA Ops:
  7.2 49.1 %all-gather.11.cloned.1.call-start = ((), (), s32[]{:S(2)}) async-start(), calls=%async_computation.9 | async-start | bytes 3170304 | tf_op jit(solution)/shard_map/all_gather | solution.py:128
  7.9 86.8 %all-gather.13.cloned.1.call-start = ((), (), s32[]{:S(2)}) async-start(), calls=%async_computation.10 | async-start | bytes 3342336 | tf_op jit(solution)/shard_map/all_gather | solution.py:124
  8.7 155.4 %all-gather.15.cloned.1.call-start = ((), (), s32[]{:S(2)}) async-start(), calls=%async_computation.11 | async-start | bytes 1114112 | tf_op jit(solution)/shard_map/all_gather | solution.py:125
  9.4 168.4 %reduce-scatter.14.cloned.1.call-start = ((), (), s32[]{:S(2)}) async-start(), calls=%async_computation.12 | async-start | bytes 3170304 | tf_op jit(solution)/shard_map/reduce_scatter | solution.py:71
  54.2 46.4 %copy-start.48 = (f32[1,1024]{1,0:T(1,128)}, f32[1,1024]{1,0:T(1,128)S(1)}, u32[]{:S(2)}) copy-start(f32[1,1024]{1,0:T(1,128)S(1)} %get-tuple-element.224) | copy-start | bytes 12292
  54.2 46.4 %copy-start.57 = (f32[1,1024]{1,0:T(1,128)}, f32[1,1024]{1,0:T(1,128)S(1)}, u32[]{:S(2)}) copy-start(f32[1,1024]{1,0:T(1,128)S(1)} %get-tuple-element.223) | copy-start | bytes 12292
  58.5 42.1 %copy-start.30 = (f32[1025]{0:T(1024)}, f32[1025]{0:T(1024)S(1)}, u32[]{:S(2)}) copy-start(f32[1025]{0:T(1024)S(1)} %broadcast_multiply_fusion.10) | copy-start | bytes 12304
  59.3 41.4 %copy-start.34 = (f32[1025]{0:T(1024)}, f32[1025]{0:T(1024)S(1)}, u32[]{:S(2)}) copy-start(f32[1025]{0:T(1024)S(1)} %add_rsqrt_fusion.2) | copy-start | bytes 12304
  164.1 13.8 copy-start.8
  169.4 55.8 %all-gather.17.cloned.1.call-start = ((), (), s32[]{:S(2)}) async-start(), calls=%async_computation.13 | async-start | bytes 3170304 | tf_op jit(solution)/shard_map/all_gather | solution.py:167
  169.7 13.6 copy-start.46
  177.9 46.7 %copy-start.54 = (bf16[1365]{0:T(1024)(128)(2,1)S(1)}, bf16[1365]{0:T(1024)(128)(2,1)}, u32[]{:S(2)}) copy-start(bf16[1365]{0:T(1024)(128)(2,1)} %param.36) | copy-start | bytes 8194
  177.9 46.7 %copy-start.55 = (bf16[1365]{0:T(1024)(128)(2,1)S(1)}, bf16[1365]{0:T(1024)(128)(2,1)}, u32[]{:S(2)}) copy-start(bf16[1365]{0:T(1024)(128)(2,1)} %param.37) | copy-start | bytes 8194
  180.5 81.9 %all-gather.19.cloned.1.call-start = ((), (), s32[]{:S(2)}) async-start(), calls=%async_computation.14 | async-start | bytes 3063808 | tf_op jit(solution)/shard_map/all_gather | solution.py:171
  181.1 148.8 %all-gather.21.cloned.1.call-start = ((), (), s32[]{:S(2)}) async-start(), calls=%async_computation.15 | async-start | bytes 3063808 | tf_op jit(solution)/shard_map/all_gather | solution.py:172
  181.8 166.7 %all-gather.25.cloned.1.call-start = ((), (), s32[]{:S(2)}) async-start(), calls=%async_computation.18 | async-start | bytes 3170304 | tf_op jit(solution)/shard_map/all_gather | solution.py:202
  182.6 228.1 %all-gather.23.cloned.1.call-start = ((), (), s32[]{:S(2)}) async-start(), calls=%async_computation.16 | async-start | bytes 3063808 | tf_op jit(solution)/shard_map/all_gather | solution.py:173
  183.3 281.8 %all-reduce.5.cloned.1.call-start = ((), (), s32[]{:S(2)}) async-start(), calls=%async_computation.19 | async-start | bytes 4227072 | tf_op jit(solution)/shard_map/psum | solution.py:77
  224.6 200.5 %copy-start.42 = (f32[1365]{0:T(1024)}, f32[1365]{0:T(1024)S(1)}, u32[]{:S(2)}) copy-start(f32[1365]{0:T(1024)S(1)} %convert_element_type.190) | copy-start | bytes 16384
  225.2 104.7 %copy-start.59 = (f32[1,1024]{1,0:T(1,128)}, f32[1,1024]{1,0:T(1,128)S(1)}, u32[]{:S(2)}) copy-start(f32[1,1024]{1,0:T(1,128)S(1)} %get-tuple-element.220) | copy-start | bytes 12292
  225.2 243.5 %copy-start.38 = (f32[1,1024]{1,0:T(1,128)}, f32[1,1024]{1,0:T(1,128)S(1)}, u32[]{:S(2)}) copy-start(f32[1,1024]{1,0:T(1,128)S(1)} %get-tuple-element.221) | copy-start | bytes 12292
  227.5 241.3 %copy-start.28 = (f32[1025]{0:T(1024)}, f32[1025]{0:T(1024)S(1)}, u32[]{:S(2)}) copy-start(f32[1025]{0:T(1024)S(1)} %broadcast_multiply_fusion.9) | copy-start | bytes 12304
  228.2 240.6 %copy-start.36 = (f32[1025]{0:T(1024)}, f32[1025]{0:T(1024)S(1)}, u32[]{:S(2)}) copy-start(f32[1025]{0:T(1024)S(1)} %add_rsqrt_fusion.1) | copy-start | bytes 12304
  342.6 82.5 %copy-start.32 = (f32[1025]{0:T(1024)}, f32[1025]{0:T(1024)S(1)}, u32[]{:S(2)}) copy-start(f32[1025]{0:T(1024)S(1)} %broadcast_multiply_fusion.4) | copy-start | bytes 12304
  348.5 76.6 %copy-start.44 = (f32[1025]{0:T(1024)}, f32[1025]{0:T(1024)S(1)}, u32[]{:S(2)}) copy-start(f32[1025]{0:T(1024)S(1)} %add_rsqrt_fusion) | copy-start | bytes 12304
  425.1 11.2 copy-start.65
  444.9 182.5 %all-reduce.7.cloned.1.call-start = ((), (), s32[]{:S(2)}) async-start(), calls=%async_computation.20 | async-start | bytes 4227072 | tf_op jit(solution)/shard_map/psum | solution.py:77
  475.8 103.7 %copy-start.23 = (f32[1025,64]{0,1:T(8,128)S(1)}, f32[1025,64]{0,1:T(8,128)}, u32[]{:S(2)}) copy-start(f32[1025,64]{0,1:T(8,128)} %get-tuple-element.212) | copy-start | bytes 787204
  576.5 6.5 copy-start.11
  594.0 5.9 copy-start.17
  594.0 5.9 copy-start.64
  604.8 155.1 %reduce-scatter.30.cloned.1.call-start = ((), (), s32[]{:S(2)}) async-start(), calls=%async_computation.27 | async-start | bytes 557056
  605.9 21.5 %copy-start.31 = (f32[1025]{0:T(1024)S(1)}, f32[1025]{0:T(1024)}, u32[]{:S(2)}) copy-start(f32[1025]{0:T(1024)} %copy-done.30) | copy-start | bytes 12304
  605.9 21.5 %copy-start.35 = (f32[1025]{0:T(1024)S(1)}, f32[1025]{0:T(1024)}, u32[]{:S(2)}) copy-start(f32[1025]{0:T(1024)} %copy-done.34) | copy-start | bytes 12304
  605.9 21.5 %copy-start.49 = (f32[1,1024]{1,0:T(1,128)S(1)}, f32[1,1024]{1,0:T(1,128)}, u32[]{:S(2)}) copy-start(f32[1,1024]{1,0:T(1,128)} %copy-done.48) | copy-start | bytes 12292
  605.9 161.1 %reduce-scatter.16.cloned.1.call-start = ((), (), s32[]{:S(2)}) async-start(), calls=%async_computation.17 | async-start | bytes 3170304 | tf_op jit(solution)/shard_map/reduce_scatter | solution.py:71
  614.5 12.9 copy-start.4
  614.5 183.0 %reduce-scatter.28.cloned.1.call-start = ((), (), s32[]{:S(2)}) async-start(), calls=%async_computation.26 | async-start | bytes 557056
  634.9 5.9 copy-start.1
  634.9 5.9 copy-start.29
  635.0 5.9 copy-start.37
  635.0 5.9 copy-start.39
  635.0 5.9 copy-start.60
  635.0 243.2 %reduce-scatter.20.cloned.1.call-start = ((), (), s32[]{:S(2)}) async-start(), calls=%async_computation.22 | async-start | bytes 2228224 | tf_op jit(solution)/shard_map/reduce_scatter | solution.py:317
  640.7 362.0 %reduce-scatter.22.cloned.1.call-start = ((), (), s32[]{:S(2)}) async-start(), calls=%async_computation.23 | async-start | bytes 6127616 | tf_op jit(solution)/shard_map/reduce_scatter | solution.py:242
  649.6 483.6 %reduce-scatter.24.cloned.1.call-start = ((), (), s32[]{:S(2)}) async-start(), calls=%async_computation.24 | async-start | bytes 6127616 | tf_op jit(solution)/shard_map/reduce_scatter | solution.py:243
  657.8 605.2 %reduce-scatter.26.cloned.1.call-start = ((), (), s32[]{:S(2)}) async-start(), calls=%async_computation.25 | async-start | bytes 6127616 | tf_op jit(solution)/shard_map/reduce_scatter | solution.py:244
  668.6 734.4 %reduce-scatter.18.cloned.1.call-start = ((), (), s32[]{:S(2)}) async-start(), calls=%async_computation.21 | async-start | bytes 6684672 | tf_op jit(solution)/shard_map/reduce_scatter | solution.py:316
  (39 other events, 112.4 us)
Sparse Core Ops, SparseCore 0:
  9.5 13.3 all-gather.10
  25.6 69.0 all-gather.12
  97.5 53.7 all-gather.14
  169.5 8.2 reduce-scatter.13
  180.6 11.8 all-gather.16
  195.1 67.2 all-gather.18
  265.2 64.6 all-gather.20
  331.4 9.2 all-gather.24
  343.5 67.1 all-gather.22
  445.0 20.0 all-reduce.4
  604.9 22.4 all-reduce.6
  629.5 78.7 reduce-scatter.29
  710.5 5.9 reduce-scatter.15
  718.6 78.8 reduce-scatter.27
  800.2 77.8 reduce-scatter.19
  880.9 121.8 reduce-scatter.21
  1005.5 127.6 reduce-scatter.23
  1135.9 126.9 reduce-scatter.25
  1265.8 137.1 reduce-scatter.17
where the time goes:
time: 1420 us; the launch traced here: 1410 us
  waiting for transfers between devices  855 us (60%)
  matrix products  225 us (16%)
  blocking collectives  169 us (12%)
  other arithmetic  81.7 us (6%)
  local copies, waits for them, and re-layouts  63.2 us (4%)
  between operations  15 us (1%)
    reduce_scatter x1, waiting for transfers between devices, body(): lax.psum_scatter(qkv_weight_grad, 'row', scatter_dimension=0, tiled=True)  140 us
    reduce_scatter x1, waiting for transfers between devices, body(): lax.psum_scatter(up_weight_grad, 'row', scatter_dimension=0, tiled=True)  130 us
    reduce_scatter x1, waiting for transfers between devices, body(): lax.psum_scatter(down_weight_grad, 'row', scatter_dimension=1, tiled=True)  130 us
    reduce_scatter x1, waiting for transfers between devices, body(): lax.psum_scatter(gate_weight_grad, 'row', scatter_dimension=0, tiled=True)  125 us
    reduce_scatter x1, waiting for transfers between devices, body(): lax.psum_scatter(proj_weight_grad, 'row', scatter_dimension=1, tiled=True)  77.9 us
    psum x1, blocking collectives, body(): lax.psum((jnp.stack([query_bias_grad, value_bias_grad]), jnp.stack([gate_...  77.1 us
    all_gather x1, waiting for transfers between devices, body(): lax.all_gather(down_weight, 'row', axis=1, tiled=True)  62.1 us
    all_gather x1, waiting for transfers between devices, body(): lax.all_gather(up_weight, 'row', axis=0, tiled=True)  59.7 us
  transfers between devices with their start and end apart: 19, of which 13 were waited for; matrix products, arithmetic and copies ran while one was open for 13% of the time, Pallas kernels for 0%

commit v1 on v0

--- a/solution.py
+++ b/solution.py
@@ -1,3 +1,4 @@
+import functools
 import math
 
 import jax
@@ -81,7 +82,30 @@
     return lax.psum(row_sums, "col")
 
 
+def lane_round(width):
+    return -(-width // 128) * 128
+
+
+def pack(pieces):
+    offsets = []
+    padded = []
+    position = 0
+    for piece in pieces:
+        width = lane_round(piece.shape[1])
+        offsets.append(position)
+        padded.append(jnp.pad(piece, ((0, 0), (0, width - piece.shape[1]))))
+        position += width
+    return jnp.concatenate(padded, axis=1), offsets
+
+
+def spread(vector, rows_local, row_count):
+    cols = -(-vector.shape[0] // rows_local)
+    block = jnp.pad(vector, (0, rows_local * cols - vector.shape[0])).reshape(rows_local, cols)
+    return jnp.tile(block, (row_count, 1))
+
+
 def body(
+    row_count,
     tokens,
     norm1_gain,
     norm1_bias,
@@ -106,6 +130,9 @@
     narrow = jnp.bfloat16
     local_rows = tokens.shape[0]
     half_width = tokens.shape[1]
+    rows_local = norm1_gain.shape[0]
+    model_width = rows_local * row_count
+    ff_local = gate_weight.shape[1]
     head_local = half_width // HD
     images_local = local_rows // SEQ
     column = lax.axis_index("col")
@@ -120,14 +147,23 @@
         shaped = array.reshape(images_local, head_local, SEQ, HD).transpose(0, 2, 1, 3)
         return shaped.reshape(local_rows, half_width)
 
-    qkv_full, proj_full, attn_vectors = (
-        lax.all_gather(qkv_weight, "row", axis=0, tiled=True),
-        lax.all_gather(proj_weight, "row", axis=1, tiled=True),
-        lax.all_gather(jnp.stack([norm1_gain, norm1_bias, proj_bias]), "row", axis=1, tiled=True),
-    )
+    attn_pack, attn_at = pack(
+        [
+            qkv_weight.reshape(rows_local, 3 * half_width),
+            proj_weight.T,
+            jnp.stack([norm1_gain, norm1_bias, proj_bias], axis=1),
+        ]
+    )
+    attn_full = lax.all_gather(attn_pack, "row", axis=0, tiled=True)
+    qkv_full = attn_full[:, attn_at[0] : attn_at[0] + 3 * half_width].reshape(
+        model_width, 3, half_width
+    )
+    proj_t = attn_full[:, attn_at[1] : attn_at[1] + half_width]
+    attn_vectors = attn_full[:, attn_at[2] : attn_at[2] + 3].astype(single)
+
     whole_input = lax.all_gather(tokens, "col", axis=1, tiled=True).astype(single)
     normed_out, normed_one, inv_std_one = norm_forward(
-        whole_input, attn_vectors[0].astype(single), attn_vectors[1].astype(single)
+        whole_input, attn_vectors[:, 0], attn_vectors[:, 1]
     )
     first_input = normed_out.astype(narrow)
     qkv_bias = jnp.stack(
@@ -158,23 +194,32 @@
     attended = from_head(
         lax.map(attend, (by_head(queries), by_head(keys_all), by_head(values_all)))
     )
-    attn_partial = jnp.dot(attended, proj_full, preferred_element_type=single)
+    attn_partial = jnp.einsum("te,de->td", attended, proj_t, preferred_element_type=single)
     residual_half = (
         tokens.astype(single)
         + share_columns(attn_partial)
-        + own_half(attn_vectors[2].astype(single), column, half_width)
+        + own_half(attn_vectors[:, 2], column, half_width)
     )
     residual_full = lax.all_gather(
         residual_half.astype(jnp.bfloat16), "col", axis=1, tiled=True
     ).astype(residual_half.dtype)
-    gate_full, up_full, down_full, ffn_vectors = (
-        lax.all_gather(gate_weight, "row", axis=0, tiled=True),
-        lax.all_gather(up_weight, "row", axis=0, tiled=True),
-        lax.all_gather(down_weight, "row", axis=1, tiled=True),
-        lax.all_gather(jnp.stack([norm2_gain, norm2_bias, down_bias]), "row", axis=1, tiled=True),
-    )
+
+    ffn_pack, ffn_at = pack(
+        [
+            gate_weight,
+            up_weight,
+            down_weight.T,
+            jnp.stack([norm2_gain, norm2_bias, down_bias], axis=1),
+        ]
+    )
+    ffn_full = lax.all_gather(ffn_pack, "row", axis=0, tiled=True)
+    gate_full = ffn_full[:, ffn_at[0] : ffn_at[0] + ff_local]
+    up_full = ffn_full[:, ffn_at[1] : ffn_at[1] + ff_local]
+    down_t = ffn_full[:, ffn_at[2] : ffn_at[2] + ff_local]
+    ffn_vectors = ffn_full[:, ffn_at[3] : ffn_at[3] + 3].astype(single)
+
     second_out, normed_two, inv_std_two = norm_forward(
-        residual_full, ffn_vectors[0].astype(single), ffn_vectors[1].astype(single)
+        residual_full, ffn_vectors[:, 0], ffn_vectors[:, 1]
     )
     second_input = second_out.astype(narrow)
     gate_value = jnp.dot(second_input, gate_full, preferred_element_type=single) + gate_bias.astype(
@@ -193,23 +238,19 @@
     down_input = (hidden_normed * inner_gain.astype(single) + inner_bias.astype(single)).astype(
         narrow
     )
-    ffn_partial = jnp.dot(down_input, down_full, preferred_element_type=single)
+    ffn_partial = jnp.einsum("tf,df->td", down_input, down_t, preferred_element_type=single)
     layer_out = (
         residual_half
         + share_columns(ffn_partial)
-        + own_half(ffn_vectors[2].astype(single), column, half_width)
+        + own_half(ffn_vectors[:, 2], column, half_width)
     ).astype(narrow)
     out_full = lax.all_gather(cotangent, "col", axis=1, tiled=True)
     out_float = out_full.astype(single)
-    gate_back, up_back, down_back, ffn_back_vectors = (
-        lax.all_gather(gate_weight, "row", axis=0, tiled=True),
-        lax.all_gather(up_weight, "row", axis=0, tiled=True),
-        lax.all_gather(down_weight, "row", axis=1, tiled=True),
-        lax.all_gather(jnp.stack([norm2_gain, norm2_bias, down_bias]), "row", axis=1, tiled=True),
-    )
-    down_weight_grad = jnp.einsum("tf,td->fd", down_input, out_full, preferred_element_type=single)
+    down_weight_grad_t = jnp.einsum(
+        "td,tf->df", out_full, down_input, preferred_element_type=single
+    )
     down_bias_grad = jnp.sum(out_float, axis=0)
-    normed_grad = jnp.einsum("td,fd->tf", out_full, down_back, preferred_element_type=single)
+    normed_grad = jnp.einsum("td,df->tf", out_full, down_t, preferred_element_type=single)
     scaled_grad = normed_grad * inner_gain.astype(single)
     first_total, second_total = hidden_totals(
         (jnp.sum(scaled_grad, axis=1), jnp.sum(scaled_grad * hidden_normed, axis=1))
@@ -230,30 +271,34 @@
     )
     up_weight_grad = jnp.einsum("td,tf->df", second_input, up_grad, preferred_element_type=single)
     second_back = join_columns(
-        jnp.einsum("tf,df->td", gate_grad, gate_back, preferred_element_type=single)
-        + jnp.einsum("tf,df->td", up_grad, up_back, preferred_element_type=single)
+        jnp.einsum("tf,df->td", gate_grad, gate_full, preferred_element_type=single)
+        + jnp.einsum("tf,df->td", up_grad, up_full, preferred_element_type=single)
     )
     second_delta, gain_two_grad, shift_two_grad = norm_backward(
-        second_back, normed_two, inv_std_two, ffn_back_vectors[0].astype(single)
+        second_back, normed_two, inv_std_two, ffn_vectors[:, 0]
     )
     residual_grad = out_float + second_delta
-    ffn_vector_grads = jnp.stack([gain_two_grad, shift_two_grad, down_bias_grad])
-    ffn_sums = (
-        lax.psum_scatter(gate_weight_grad, "row", scatter_dimension=0, tiled=True),
-        lax.psum_scatter(up_weight_grad, "row", scatter_dimension=0, tiled=True),
-        lax.psum_scatter(down_weight_grad, "row", scatter_dimension=1, tiled=True),
-        lax.psum_scatter(ffn_vector_grads, "row", scatter_dimension=1, tiled=True),
-    )
-    qkv_back, proj_back, attn_back_vectors = (
-        lax.all_gather(qkv_weight, "row", axis=0, tiled=True),
-        lax.all_gather(proj_weight, "row", axis=1, tiled=True),
-        lax.all_gather(jnp.stack([norm1_gain, norm1_bias, proj_bias]), "row", axis=1, tiled=True),
-    )
     attn_grad = residual_grad.astype(narrow)
     proj_bias_grad = jnp.sum(attn_grad.astype(single), axis=0)
-    proj_weight_grad = jnp.einsum("te,td->ed", attended, attn_grad, preferred_element_type=single)
+    proj_weight_grad_t = jnp.einsum(
+        "td,te->de", attn_grad, attended, preferred_element_type=single
+    )
+    mid_small = jnp.concatenate([gate_bias_grad, up_bias_grad, inner_gain_grad, inner_bias_grad])
+    mid_pack, mid_at = pack(
+        [
+            gate_weight_grad.astype(narrow),
+            up_weight_grad.astype(narrow),
+            down_weight_grad_t.astype(narrow),
+            proj_weight_grad_t.astype(narrow),
+            jnp.stack(
+                [gain_two_grad, shift_two_grad, down_bias_grad, proj_bias_grad], axis=1
+            ).astype(narrow),
+            spread(mid_small, rows_local, row_count).astype(narrow),
+        ]
+    )
+    mid_sums = lax.psum_scatter(mid_pack, "row", scatter_dimension=0, tiled=True).astype(single)
     attended_grad = jnp.einsum(
-        "td,ed->te", attn_grad, proj_back, preferred_element_type=single
+        "td,de->te", attn_grad, proj_t, preferred_element_type=single
     ).astype(narrow)
 
     def attend_back(operands):
@@ -305,45 +350,50 @@
         "td,tpe->dpe", first_input, qkv_grad, preferred_element_type=single
     )
     first_back = join_columns(
-        jnp.einsum("tpe,dpe->td", qkv_grad, qkv_back, preferred_element_type=single)
+        jnp.einsum("tpe,dpe->td", qkv_grad, qkv_full, preferred_element_type=single)
     )
     first_delta, gain_one_grad, shift_one_grad = norm_backward(
-        first_back, normed_one, inv_std_one, attn_back_vectors[0].astype(single)
+        first_back, normed_one, inv_std_one, attn_vectors[:, 0]
     )
     input_grad = own_half(residual_grad + first_delta, column, half_width).astype(narrow)
-    attn_vector_grads = jnp.stack([gain_one_grad, shift_one_grad, proj_bias_grad])
-    attn_sums = (
-        lax.psum_scatter(qkv_weight_grad, "row", scatter_dimension=0, tiled=True),
-        lax.psum_scatter(proj_weight_grad, "row", scatter_dimension=1, tiled=True),
-        lax.psum_scatter(attn_vector_grads, "row", scatter_dimension=1, tiled=True),
-    )
-    small_sums = lax.psum(
-        (
-            jnp.stack([query_bias_grad, value_bias_grad]),
-            jnp.stack([gate_bias_grad, up_bias_grad, inner_gain_grad, inner_bias_grad]),
-        ),
-        "row",
-    )
+    end_pack, end_at = pack(
+        [
+            qkv_weight_grad.reshape(model_width, 3 * half_width).astype(narrow),
+            jnp.stack([gain_one_grad, shift_one_grad], axis=1).astype(narrow),
+            spread(
+                jnp.concatenate([query_bias_grad, value_bias_grad]), rows_local, row_count
+            ).astype(narrow),
+        ]
+    )
+    end_sums = lax.psum_scatter(end_pack, "row", scatter_dimension=0, tiled=True).astype(single)
+
+    def cut(sums, offset, width):
+        return sums[:, offset : offset + width]
+
+    mid_vectors = cut(mid_sums, mid_at[4], 4)
+    mid_small_sum = cut(mid_sums, mid_at[5], -(-mid_small.shape[0] // rows_local)).reshape(-1)
+    end_vectors = cut(end_sums, end_at[1], 2)
+    end_small_sum = cut(end_sums, end_at[2], -(-2 * half_width // rows_local)).reshape(-1)
     return (
         layer_out,
         input_grad,
-        attn_sums[2][0],
-        attn_sums[2][1],
-        attn_sums[0],
-        small_sums[0][0],
-        small_sums[0][1],
-        attn_sums[1],
-        attn_sums[2][2],
-        ffn_sums[3][0],
-        ffn_sums[3][1],
-        ffn_sums[0],
-        small_sums[1][0],
-        ffn_sums[1],
-        small_sums[1][1],
-        small_sums[1][2],
-        small_sums[1][3],
-        ffn_sums[2],
-        ffn_sums[3][2],
+        end_vectors[:, 0],
+        end_vectors[:, 1],
+        cut(end_sums, end_at[0], 3 * half_width).reshape(rows_local, 3, half_width),
+        end_small_sum[:half_width],
+        end_small_sum[half_width : 2 * half_width],
+        cut(mid_sums, mid_at[3], half_width).T,
+        mid_vectors[:, 3],
+        mid_vectors[:, 0],
+        mid_vectors[:, 1],
+        cut(mid_sums, mid_at[0], ff_local),
+        mid_small_sum[:ff_local],
+        cut(mid_sums, mid_at[1], ff_local),
+        mid_small_sum[ff_local : 2 * ff_local],
+        mid_small_sum[2 * ff_local : 3 * ff_local],
+        mid_small_sum[3 * ff_local : 4 * ff_local],
+        cut(mid_sums, mid_at[2], ff_local).T,
+        mid_vectors[:, 2],
     )
 
 
@@ -370,7 +420,7 @@
         P("row", "col"),
     )
     return jax.shard_map(
-        body,
+        functools.partial(body, mesh.shape["row"]),
         mesh=mesh,
         in_specs=placed,
         out_specs=(

time: 1420 us -> 899 us (0.63)
  waiting for transfers between devices: 855 us -> 453 us
  blocking collectives: 169 us -> 8.48 us
  local copies, waits for them, and re-layouts: 63.2 us -> 94.1 us
  other arithmetic: 81.7 us -> 97 us
    reduce_scatter x5 -> x1, waiting for transfers between devices: 603 us -> 36.4 us  [body(): lax.psum_scatter(end_pack, 'row', scatter_dimension=0, tiled=True)]
    unnamed x21 -> x12, waiting for transfers between devices: 32.6 us -> 179 us
    all_gather x2 -> x0, blocking collectives: 83.5 us -> none  [the longest x1 42.5 us: body(): lax.all_gather(jnp.stack([norm1_gain, norm1_bias, proj_bias]), 'row', axi...]
    psum x1 -> x0, blocking collectives: 77.1 us -> none  [body(): lax.psum((jnp.stack([query_bias_grad, value_bias_grad]), jnp.stack([gate_...]
    unnamed x146 -> x165, local copies, waits for them, and re-layouts: 14.3 us -> 31.4 us
    all_gather x5 -> x2, waiting for transfers between devices: 191 us -> 197 us  [the longest x1 118 us: body(): ffn_full = lax.all_gather(ffn_pack, 'row', axis=0, tiled=True)]
  transfers between devices with their start and end apart: 19 -> 11, of which waited for: 13 -> 8; matrix products, arithmetic and copies ran while one was open for 13% -> 15% of each run, Pallas kernels for 0% -> 0%
where the time goes in v1:
time: 899 us; the launch traced here: 887 us
  waiting for transfers between devices  453 us (50%)
  matrix products  218 us (24%)
  other arithmetic  97 us (11%)
  local copies, waits for them, and re-layouts  94.1 us (10%)
  between operations  15.5 us (2%)
    unnamed x12, waiting for transfers between devices  179 us
    all_gather x1, waiting for transfers between devices, body(): ffn_full = lax.all_gather(ffn_pack, 'row', axis=0, tiled=True)  118 us
    all_gather x1, waiting for transfers between devices, body(): attn_full = lax.all_gather(attn_pack, 'row', axis=0, tiled=True)  79.2 us
    reduce_scatter x1, waiting for transfers between devices, body(): lax.psum_scatter(end_pack, 'row', scatter_dimension=0, tiled=True)  36.4 us
    unnamed x165, local copies, waits for them, and re-layouts  31.4 us
    dot_general x8, matrix products, attend(): jnp.einsum('qk,kd->qd', weights.astype(narrow), value_block, preferred_el...  20.7 us
    dot_general x8, matrix products, attend_back(): jnp.einsum('qk,qd->kd', weights.astype(narrow), grad_block, preferred_ele...  20.2 us
    dot_general x8, matrix products, attend_back(): jnp.einsum('qk,qd->kd', score_grad, query_block, preferred_element_type=s...  20.1 us
  transfers between devices with their start and end apart: 11, of which 8 were waited for; matrix products, arithmetic and copies ran while one was open for 15% of the time, Pallas kernels for 0%

profile of v1, /device:TPU:0, one launch (start us, length us, event | category | flops | bytes accessed | tf_op | source)
XLA Modules:
  0.0 887.3 jit_solution(17714414229249242951)
XLA Ops:
  14.9 8.0 all-gather.6.cloned.1.call-done
  25.9 79.2 %all-gather.8.cloned.1.call-done = bf16[1024,2176]{1,0:T(8,128)(2,1)} async-done(((bf16[64,2176]{1,0:T(8,128)(2,1)}), bf16[1024,2176]{1,0:T(8,128)(2,1)}) %all-gather.8.cloned.1.call-update) | async-done | bytes 4456464 | tf_op jit(solution)/shard_map/all_gather | solution.py:157
  105.1 3.8 slice.169
  108.9 4.6 copy.177
  115.7 5.9 convolution_add_fusion.2
  127.1 3.0 copy.179
  134.3 2.9 copy.184
  143.6 41.5 %while.24 = (s32[]{:T(128)}, bf16[8,1025,64]{1,2,0:T(8,128)(2,1)}, bf16[8,1025,64]{2,1,0:T(8,128)(2,1)S(1)}, bf16[8,1025,64]{2,1,0:T(8,128)(2,1)}, bf16[8,1025,64]{2,1,0:T(8,128)(2,1)}, /*index=5*/s32[]{:T(128)}) while((s32[]{:T(128)}, bf16[8,1025,64]{1,2,0:T(8,128)(2,1)}, bf16[8,1025,64]{2,1,0:T(8,128)(2,1)S(1)}, ...), condition=%wide.region_5.6_spmd, body=%wide.region_2.5_spmd.sunk | while | flops 276377920 | bytes 13570157 | solution.py:195
  177.2 2.6 fusion.191
  185.1 5.2 convolution_convert_fusion.4
  191.8 7.0 reduce-scatter.7.cloned.1.call-done
  203.2 10.2 %all-gather.10.cloned.1.call-done = bf16[1025,1024]{1,0:T(8,128)(2,1)} async-done(((bf16[1025,512]{1,0:T(8,128)(2,1)}), bf16[1025,1024]{1,0:T(8,128)(2,1)}) %all-gather.10.cloned.1.call-update) | async-done | bytes 2099216 | tf_op jit(solution)/shard_map/all_gather | solution.py:203
  216.4 118.3 %all-gather.12.cloned.1.call-done = bf16[1024,4352]{1,0:T(8,128)(2,1)} async-done(((bf16[64,4352]{1,0:T(8,128)(2,1)}), bf16[1024,4352]{1,0:T(8,128)(2,1)}) %all-gather.12.cloned.1.call-update) | async-done | bytes 8912912 | tf_op jit(solution)/shard_map/all_gather | solution.py:215
  336.8 5.8 convolution_add_fusion.1
  342.6 11.1 %fusion.152 = (f32[1025]{0:T(1024)S(1)}, f32[1025,1365]{1,0:T(8,128)}, f32[1025,1365]{1,0:T(8,128)}) fusion(f32[1025,1365]{1,0:T(8,128)S(1)} %convolution_add_fusion.1, f32[1365]{0:T(1024)S(1)} %convert_element_type.241, bf16[1024,4352]{1,0:T(8,128)(2,1)} %all-gather.12.cloned.1.call-done, bf16[1025,1024]{1,0:T(8,128)(2,1)S(1)} %copy-done, ...), kind=kOutput, calls=%fused_computation.268 | convolution fusion | flops 2881498112 | bytes 21798236 | tf_op jit(solution)/shard_map/dot_general | solution.py:228
  356.3 3.4 multiply_reduce_fusion.2
  359.7 2.7 psum.43
  362.4 11.8 %fusion.51 = (bf16[1365]{0:T(1024)(128)(2,1)}, f32[1025]{0:T(1024)S(1)}, f32[1025]{0:T(1024)S(1)}, f32[1365,1025]{0,1:T(8,128)}) fusion(f32[1025,1365]{1,0:T(8,128)} %get-tuple-element.293, f32[1025]{0:T(1024)S(1)} %add_rsqrt_fusion, f32[1025]{0:T(1024)S(1)} %broadcast_multiply_fusion.4, f32[1365]{0:T(1024)S(1)} %convert_element_type.242, ...), kind=kOutput, calls=%fused_computation.62 | convolution fusion | flops 2876596992 | bytes 16430434 | tf_op jit(solution)/shard_map/td,df->tf/dot_general | solution.py:253
  374.2 3.3 all-reduce.13
  377.6 10.9 %fusion.149 = (bf16[1365]{0:T(1024)(128)(2,1)}, bf16[1025,1365]{1,0:T(8,128)(2,1)S(1)}, bf16[1365]{0:T(1024)(128)(2,1)}, bf16[1025,1365]{1,0:T(8,128)(2,1)S(1)}) fusion(f32[1025,1365]{1,0:T(8,128)} %copy-done.14, f32[1025]{0:T(1024)S(1)} %broadcast_multiply_fusion.2, f32[1025,1365]{1,0:T(8,128)} %get-tuple-element.293, ...), kind=kLoop, calls=%fused_computation.266 | loop fusion | flops 30778012 | bytes 28009820 | tf_op jit(solution)/shard_map/reduce_sum | solution.py:268
  388.5 7.4 fusion.82
  396.0 6.6 fusion.73
  404.7 3.0 copy.194
  407.7 14.7 %all-reduce.17.cloned.1.call-done = bf16[1025,1024]{1,0:T(8,128)(2,1)} async-done(((bf16[1025,1024]{1,0:T(8,128)(2,1)}), bf16[1025,1024]{1,0:T(8,128)(2,1)}) %all-reduce.17.cloned.1.call-update) | async-done | bytes 2099216 | tf_op jit(solution)/shard_map/psum | solution.py:78
  422.4 4.1 fusion.70
  426.6 3.5 convert_reduce_fusion.2
  432.1 2.6 convolution_convert_fusion.5
  436.2 100.7 %while.25 = (s32[]{:T(128)}, f32[8,1025,64]{1,2,0:T(8,128)S(1)}, f32[8,1025,64]{1,2,0:T(8,128)}, bf16[8,1025,64]{1,2,0:T(8,128)(2,1)}, bf16[8,1025,64]{2,1,0:T(8...) while((s32[]{:T(128)}, f32[8,1025,64]{1,2,0:T(8,128)S(1)}, ...), condition=%wide.region_25.26_spmd, body=%wide.region_21.25_spmd.sunk | while | flops 689338112 | bytes 38548656 | solution.py:328
  536.9 3.1 copy.199
  540.0 3.3 bitcast_multiply_fusion.3
  545.6 3.1 copy.193
  551.2 3.1 copy.196
  554.3 4.9 add_convert_fusion.3
  560.2 4.7 fusion.72
  565.1 8.6 convolution_convert_fusion
  576.2 7.8 convolution_convert_fusion.6
  584.1 4.8 copy.201
  590.9 6.3 fusion.71
  597.4 3.4 fusion.75
  601.0 3.1 reduce_sum.266
  604.7 6.8 convolution_convert_fusion.3
  613.3 4.6 convolution_convert_fusion.2
  619.8 5.6 fusion.76
  631.4 13.6 %copy.212 = bf16[1024,4992]{1,0:T(8,128)(2,1)} copy(bf16[1024,4992]{0,1:T(8,128)(2,1)} %pad_dynamic-update-slice_fusion.3) | data formatting | bytes 20447232
  646.2 4.5 fusion.90
  650.8 2.7 add_convert_fusion.4
  653.5 36.4 %reduce-scatter.11.cloned.1.call-done = bf16[64,1792]{1,0:T(8,128)(2,1)} async-done(((bf16[1024,1792]{1,0:T(8,128)(2,1)}), bf16[64,1792]{1,0:T(8,128)(2,1)}) %reduce-scatter.11.cloned.1.call-update) | async-done | bytes 229392 | tf_op jit(solution)/shard_map/reduce_scatter | solution.py:368
  695.4 177.4 %reduce-scatter.13.cloned.1.call-done = bf16[64,4992]{1,0:T(8,128)(2,1)} async-done(((bf16[1024,4992]{1,0:T(8,128)(2,1)}), bf16[64,4992]{1,0:T(8,128)(2,1)}) %reduce-scatter.13.cloned.1.call-update) | async-done | bytes 638992
  (370 shorter events, 221.6 us)
Async XLA Ops:
  7.2 15.7 %all-gather.6.cloned.1.call-start = ((), (), s32[]{:S(2)}) async-start(), calls=%async_computation.4 | async-start | bytes 3170304 | tf_op jit(solution)/shard_map/all_gather | solution.py:164
  7.9 97.1 %all-gather.8.cloned.1.call-start = ((), (), s32[]{:S(2)}) async-start(), calls=%async_computation.5 | async-start | bytes 4734976 | tf_op jit(solution)/shard_map/all_gather | solution.py:157
  11.3 187.5 %reduce-scatter.7.cloned.1.call-start = ((), (), s32[]{:S(2)}) async-start(), calls=%async_computation.6 | async-start | bytes 3170304 | tf_op jit(solution)/shard_map/reduce_scatter | solution.py:72
  25.1 90.5 %copy-start.36 = (f32[1025]{0:T(1024)}, f32[1025]{0:T(1024)S(1)}, u32[]{:S(2)}) copy-start(f32[1025]{0:T(1024)S(1)} %broadcast_multiply_fusion.10) | copy-start | bytes 12304
  25.9 89.8 %copy-start.42 = (f32[1025]{0:T(1024)}, f32[1025]{0:T(1024)S(1)}, u32[]{:S(2)}) copy-start(f32[1025]{0:T(1024)S(1)} %add_rsqrt_fusion.2) | copy-start | bytes 12304
  115.6 5.9 copy-start.52
  115.6 5.9 copy-start.60
  185.1 13.7 %copy-start.7 = (bf16[1025,512]{1,0:T(8,128)(2,1)S(1)}, bf16[1025,512]{1,0:T(8,128)(2,1)}, u32[]{:S(2)}) copy-start(bf16[1025,512]{1,0:T(8,128)(2,1)} %param.23) | copy-start | bytes 3148804
  190.3 11.1 %copy-start.69 = (bf16[64]{0:T(256)(128)(2,1)S(1)}, bf16[64]{0:T(256)(128)(2,1)}, u32[]{:S(2)}) copy-start(bf16[64]{0:T(256)(128)(2,1)} %param.40) | copy-start | bytes 388
  190.3 11.1 %copy-start.70 = (bf16[64]{0:T(256)(128)(2,1)S(1)}, bf16[64]{0:T(256)(128)(2,1)}, u32[]{:S(2)}) copy-start(bf16[64]{0:T(256)(128)(2,1)} %param.32) | copy-start | bytes 388
  190.3 11.1 %copy-start.71 = (bf16[64]{0:T(256)(128)(2,1)S(1)}, bf16[64]{0:T(256)(128)(2,1)}, u32[]{:S(2)}) copy-start(bf16[64]{0:T(256)(128)(2,1)} %param.31) | copy-start | bytes 388
  190.3 11.2 %copy-start.31 = (bf16[1365,64]{0,1:T(8,128)(2,1)S(1)}, bf16[1365,64]{0,1:T(8,128)(2,1)}, u32[]{:S(2)}) copy-start(bf16[1365,64]{0,1:T(8,128)(2,1)} %param.39) | copy-start | bytes 524164
  190.4 11.2 %copy-start.32 = (bf16[64,1365]{1,0:T(8,128)(2,1)S(1)}, bf16[64,1365]{1,0:T(8,128)(2,1)}, u32[]{:S(2)}) copy-start(bf16[64,1365]{1,0:T(8,128)(2,1)} %param.35) | copy-start | bytes 524164
  190.4 11.2 %copy-start.33 = (bf16[64,1365]{1,0:T(8,128)(2,1)S(1)}, bf16[64,1365]{1,0:T(8,128)(2,1)}, u32[]{:S(2)}) copy-start(bf16[64,1365]{1,0:T(8,128)(2,1)} %param.33) | copy-start | bytes 524164
  190.4 23.0 %all-gather.10.cloned.1.call-start = ((), (), s32[]{:S(2)}) async-start(), calls=%async_computation.7 | async-start | bytes 3170304 | tf_op jit(solution)/shard_map/all_gather | solution.py:203
  191.7 9.7 %copy-start.50 = (f32[512]{0:T(512)}, f32[512]{0:T(512)S(1)}, u32[]{:S(2)}) copy-start(f32[512]{0:T(512)S(1)} %dynamic-slice_reduce_fusion.1) | copy-start | bytes 6148
  191.7 11.4 %copy-start.64 = (bf16[1365]{0:T(1024)(128)(2,1)S(1)}, bf16[1365]{0:T(1024)(128)(2,1)}, u32[]{:S(2)}) copy-start(bf16[1365]{0:T(1024)(128)(2,1)} %param.34) | copy-start | bytes 8194
  191.7 11.4 %copy-start.65 = (bf16[1365]{0:T(1024)(128)(2,1)S(1)}, bf16[1365]{0:T(1024)(128)(2,1)}, u32[]{:S(2)}) copy-start(bf16[1365]{0:T(1024)(128)(2,1)} %param.36) | copy-start | bytes 8194
  191.8 11.4 %copy-start.66 = (bf16[1365]{0:T(1024)(128)(2,1)S(1)}, bf16[1365]{0:T(1024)(128)(2,1)}, u32[]{:S(2)}) copy-start(bf16[1365]{0:T(1024)(128)(2,1)} %param.37) | copy-start | bytes 8194
  201.4 133.3 %all-gather.12.cloned.1.call-start = ((), (), s32[]{:S(2)}) async-start(), calls=%async_computation.8 | async-start | bytes 9469952 | tf_op jit(solution)/shard_map/all_gather | solution.py:215
  202.5 159.9 %all-gather.14.cloned.1.call-start = ((), (), s32[]{:S(2)}) async-start(), calls=%async_computation.10 | async-start | bytes 3170304 | tf_op jit(solution)/shard_map/all_gather | solution.py:247
  203.0 219.4 %all-reduce.17.cloned.1.call-start = ((), (), s32[]{:S(2)}) async-start(), calls=%async_computation.11 | async-start | bytes 4227072 | tf_op jit(solution)/shard_map/psum | solution.py:78
  203.2 174.4 %copy-start.46 = (f32[1365]{0:T(1024)}, f32[1365]{0:T(1024)S(1)}, u32[]{:S(2)}) copy-start(f32[1365]{0:T(1024)S(1)} %convert_element_type.242) | copy-start | bytes 16384
  215.6 211.0 %copy-start.34 = (f32[1025]{0:T(1024)}, f32[1025]{0:T(1024)S(1)}, u32[]{:S(2)}) copy-start(f32[1025]{0:T(1024)S(1)} %broadcast_multiply_fusion.9) | copy-start | bytes 12304
  216.3 210.2 %copy-start.38 = (f32[1025]{0:T(1024)}, f32[1025]{0:T(1024)S(1)}, u32[]{:S(2)}) copy-start(f32[1025]{0:T(1024)S(1)} %add_rsqrt_fusion.1) | copy-start | bytes 12304
  336.8 89.8 %copy-start.44 = (f32[1024]{0:T(1024)}, f32[1024]{0:T(1024)S(1)}, u32[]{:S(2)}) copy-start(f32[1024]{0:T(1024)S(1)} %get-tuple-element.252) | copy-start | bytes 12292
  342.6 11.2 %copy-start.14 = (f32[1025,1365]{1,0:T(8,128)}, f32[1025,1365]{1,0:T(8,128)S(1)}, u32[]{:S(2)}) copy-start(f32[1025,1365]{1,0:T(8,128)S(1)} %convolution_add_fusion.1) | copy-start | bytes 16789504
  356.3 21.3 %copy-start.40 = (f32[1025]{0:T(1024)}, f32[1025]{0:T(1024)S(1)}, u32[]{:S(2)}) copy-start(f32[1025]{0:T(1024)S(1)} %broadcast_multiply_fusion.4) | copy-start | bytes 12304
  362.4 15.2 %copy-start.48 = (f32[1025]{0:T(1024)}, f32[1025]{0:T(1024)S(1)}, u32[]{:S(2)}) copy-start(f32[1025]{0:T(1024)S(1)} %add_rsqrt_fusion) | copy-start | bytes 12304
  388.5 7.4 copy-start.23
  388.5 7.4 copy-start.21
  395.9 7.2 copy-start.27
  402.6 186.3 %all-reduce.19.cloned.1.call-start = ((), (), s32[]{:S(2)}) async-start(), calls=%async_computation.12 | async-start | bytes 4227072 | tf_op jit(solution)/shard_map/psum | solution.py:78
  436.2 103.8 %copy-start.25 = (f32[1025,64]{0,1:T(8,128)S(1)}, f32[1025,64]{0,1:T(8,128)}, u32[]{:S(2)}) copy-start(f32[1025,64]{0,1:T(8,128)} %get-tuple-element.341) | copy-start | bytes 787204
  536.9 6.5 copy-start.10
  554.3 5.9 copy-start.17
  554.3 5.9 copy-start.20
  565.0 85.8 %reduce-scatter.9.cloned.1.call-start = ((), (), s32[]{:S(2)}) async-start(), calls=%async_computation.9 | async-start | bytes 3170304 | tf_op jit(solution)/shard_map/reduce_scatter | solution.py:72
  565.1 8.9 copy-start.16
  565.1 8.9 copy-start.18
  573.7 116.3 %reduce-scatter.11.cloned.1.call-start = ((), (), s32[]{:S(2)}) async-start(), calls=%async_computation.13 | async-start | bytes 3899392 | tf_op jit(solution)/shard_map/reduce_scatter | solution.py:368
  600.9 271.9 %reduce-scatter.13.cloned.1.call-start = ((), (), s32[]{:S(2)}) async-start(), calls=%async_computation.14 | async-start | bytes 10862592
  604.7 8.6 copy-start.22
  611.4 8.3 slice-start
  613.3 6.5 slice-start.1
  613.3 6.5 copy-start.29
  617.9 9.5 %slice-start.2 = ((s8[4227072]{0:T(1024)(128)(4,1)}), s8[4194304]{0:T(1024)(128)(4,1)S(1)}, s32[]{:S(2)}) async-start(s8[4227072]{0:T(1024)(128)(4,1)} %bitcast.235), calls=%async_computation.17 | async-start | bytes 8388608
  619.8 7.6 slice-start.3
  (40 other events, 125.3 us)
Sparse Core Ops, SparseCore 0:
  9.5 13.3 all-gather.5
  26.2 78.7 all-gather.7
  190.5 8.2 reduce-scatter.6
  201.5 11.8 all-gather.9
  216.5 118.1 all-gather.11
  336.1 8.7 all-gather.13
  402.7 19.6 all-reduce.16
  565.1 22.5 all-reduce.18
  589.9 10.8 reduce-scatter.8
  602.9 86.9 reduce-scatter.10
  695.7 177.0 reduce-scatter.12
